TPU v7x, 256 devices: a whole 4x4x8 slice. The times are simulated.
256 devices in a mesh: section: 4 (over x_hi, core), dp: 64 (over y, x_lo, z).
Axes of the slice: x: 4 (x_hi: 2, x_lo: 2; x = x_hi * 2 + x_lo), y: 4, z: 8, core: 2. Of those that a mesh axis runs over, the one named last changes fastest.
Arguments:
- activations: bfloat16 [12288, 8, 4096], P('dp', 'section'), may hold values from -8 to 8
- damping: float32 [8], P('section'), may hold values from 0.1 to 1
Outputs:
- schur_inverse: float32 [256, 128, 128], P(('section', 'dp'))
- coupling: float32 [256, 128, 128], P(('section', 'dp'))
All inputs are finite; a program needn't handle non-finite values.
Results may differ from a plain program's by a relative error of at most 0.0003.
Values may be sent and summed in bfloat16 or wider, within the bound.
A program may use at most 64 MiB of HBM per device.

v0:
```python
import jax
import jax.numpy as jnp
from jax import lax
from jax.sharding import PartitionSpec as P

B = 128


def passed_along(block, axis, distance):
    devices = range(lax.axis_size(axis))
    route = [(i - distance, i) for i in devices if i - distance in devices]
    return lax.ppermute(block, axis, route)


def sent_to_all(array, axis):
    copies = jnp.broadcast_to(array, (lax.axis_size(axis), *array.shape))
    return lax.all_to_all(copies, axis, split_axis=0, concat_axis=0, tiled=True)


def over_copies(array, axis):
    everything = sent_to_all(array, axis)
    return jnp.sum(everything, axis=0)


def solve_block(system, right_side):
    factor = jnp.linalg.cholesky(system)
    return jax.scipy.linalg.cho_solve((factor, True), right_side)


def local(activations, damping):
    token_rows, local_layers, model_width = activations.shape
    block_size = B
    blocks_layer = model_width // block_size
    group_size = lax.axis_size("dp")
    section_count = lax.axis_size("section")
    per_device = local_layers * blocks_layer // group_size
    tokens_all = token_rows * group_size
    flattened = activations.reshape(token_rows, local_layers * model_width)
    following_rows = passed_along(flattened[:, :model_width], "section", -1)
    next_layers = jnp.concatenate([flattened[:, model_width:], following_rows], axis=1)
    owner_layer = lax.axis_index("dp") * per_device // blocks_layer
    layer_index = jnp.arange(local_layers)
    sent_pairs = (
        flattened.reshape(token_rows, group_size, per_device * block_size),
        next_layers.reshape(token_rows, group_size, per_device * block_size),
    )
    left_cols, right_cols = (
        lax.all_to_all(sent_pairs[0], "dp", split_axis=1, concat_axis=0, tiled=True),
        lax.all_to_all(sent_pairs[1], "dp", split_axis=1, concat_axis=0, tiled=True),
    )
    diagonal_gram = (
        jnp.einsum("tgb,tgc->gbc", left_cols, left_cols, preferred_element_type=jnp.float32)
        / tokens_all
    )
    cross_gram = (
        jnp.einsum("tgb,tgc->gbc", left_cols, right_cols, preferred_element_type=jnp.float32)
        / tokens_all
    )
    owned_trace = jnp.sum(jnp.trace(diagonal_gram, axis1=1, axis2=2))
    traces = over_copies(jnp.where(layer_index == owner_layer, owned_trace, 0.0), "dp")
    identity = jnp.eye(block_size, dtype=jnp.float32)
    damp_level = jnp.sum(jnp.where(layer_index == owner_layer, traces * damping, 0.0)) / model_width
    damped = diagonal_gram + damp_level * identity
    following_damped = passed_along(damped, ("section", "dp"), -(group_size // local_layers))
    final_layer = jnp.logical_and(
        lax.axis_index("section") == section_count - 1, owner_layer == local_layers - 1
    )
    system = jnp.where(final_layer, identity, following_damped)
    cross_gram = jnp.where(final_layer, jnp.zeros_like(cross_gram), cross_gram)
    coupling_t = jax.vmap(solve_block)(system, jnp.swapaxes(cross_gram, 1, 2))
    schur = damped - jnp.matmul(cross_gram, coupling_t, precision=lax.Precision.HIGHEST)
    identities = jnp.broadcast_to(identity, schur.shape)
    schur_inverse = jax.vmap(solve_block)(schur, identities)
    return (schur_inverse, jnp.swapaxes(coupling_t, 1, 2))


def solution(mesh):
    placed = (P("dp", "section", None), P("section"))
    return jax.shard_map(
        local,
        mesh=mesh,
        in_specs=placed,
        out_specs=(P(("section", "dp"), None, None), P(("section", "dp"), None, None)),
        check_vma=False,
    )
```

profile of v0, /device:TPU:4, one launch (start us, length us, event | category | flops | bytes accessed | tf_op | source)
XLA Modules:
  0.0 224.7 jit_solution(8540265799306868774)
XLA Ops:
  0.6 4.8 %reshape_reshape.3 = bf16[192,64,128]{2,1,0:T(8,128)(2,1)S(1)} reshape(bf16[192,2,4096]{2,1,0:T(2,128)(2,1)} %param.5) | data formatting | bytes 6291456 | tf_op jit(solution)/shard_map/reshape;reshape | solution.py:44
  5.4 3.7 %copy.26 = bf16[192,64,128]{2,0,1:T(8,128)(2,1)} copy(bf16[192,64,128]{2,1,0:T(8,128)(2,1)S(1)} %reshape_reshape.3) | data formatting | bytes 6291456 | tf_op jit(solution)/shard_map/reshape;reshape | solution.py:44
  9.2 13.2 %all-to-all-start = ((bf16[192,64,128]{2,0,1:T(8,128)(2,1)}), bf16[192,64,128]{2,0,1:T(8,128)(2,1)}, u32[]{:S(2)}, u32[]{:S(2)}) async-start(bf16[192,64,128]{2,0,1:T(8,128)(2,1)} %copy.26), calls=%async_computation | async-start | bytes 6291456 | tf_op jit(solution)/shard_map/all_to_all | solution.py:48
  22.4 2.1 copy.42
  24.5 0.2 fusion.41
  24.7 1.9 collective-permute-start
  26.7 70.0 %all-to-all-done = bf16[192,64,128]{2,0,1:T(8,128)(2,1)} async-done(((bf16[192,64,128]{2,0,1:T(8,128)(2,1)}), bf16[192,64,128]{2,0,1:T(8,128)(2,1)}, u32[]{:S(2)}, u32[]{:S(2)}) %all-to-all-start) | async-done | bytes 3145760 | tf_op jit(solution)/shard_map/all_to_all | solution.py:48
  96.7 4.5 %select_reduce_fusion.1 = (f32[]{:T(128)}, f32[128,128]{0,1:T(8,128)S(1)}) fusion(bf16[192,64,128]{2,0,1:T(8,128)(2,1)} %all-to-all-done), kind=kOutput, calls=%fused_computation.38 | convolution fusion | flops 402718720 | bytes 3211268 | tf_op jit(solution)/shard_map/tgb,tgc->gbc/dot_general | solution.py:52
  101.2 0.6 compare_select_fusion.1
  101.8 0.6 broadcast_in_dim.31
  102.5 5.5 %all-to-all-start.1 = ((f32[64,1,2]{2,1,0:T(1,128)}), f32[64,1,2]{2,1,0:T(1,128)S(1)}, u32[]{:S(2)}, u32[]{:S(2)}) async-start(f32[64,1,2]{2,1,0:T(1,128)} %broadcast_in_dim.31), calls=%async_computation.1 | async-start | bytes 65536 | tf_op jit(solution)/shard_map/all_to_all | solution.py:17
  108.0 4.0 %copy_bitcast_fusion = bf16[192,64,128]{2,0,1:T(8,128)(2,1)} fusion(bf16[192,4096]{1,0:T(8,128)(2,1)} %collective-permute-done, bf16[192,4096]{1,0:T(8,128)(2,1)S(1)} %get-tuple-element.12), kind=kLoop, calls=%fused_computation | loop fusion | flops 6291456 | bytes 6291456 | tf_op jit(solution)/shard_map/reshape | solution.py:45
  112.0 6.3 %all-to-all-done.1 = f32[64,1,2]{2,1,0:T(1,128)S(1)} async-done(((f32[64,1,2]{2,1,0:T(1,128)}), f32[64,1,2]{2,1,0:T(1,128)S(1)}, u32[]{:S(2)}, u32[]{:S(2)}) %all-to-all-start.1) | async-done | bytes 544 | tf_op jit(solution)/shard_map/all_to_all | solution.py:17
  118.4 5.0 %all-to-all-start.2 = ((bf16[192,64,128]{2,0,1:T(8,128)(2,1)}), bf16[192,64,128]{2,0,1:T(8,128)(2,1)S(1)}, u32[]{:S(2)}, u32[]{:S(2)}) async-start(bf16[192,64,128]{2,0,1:T(8,128)(2,1)} %copy_bitcast_fusion), calls=%async_computation.2 | async-start | bytes 6291456 | tf_op jit(solution)/shard_map/all_to_all | solution.py:49
  123.5 0.6 fusion.40
  124.8 3.6 %collective-permute-start.1 = (f32[1,128,128]{1,2,0:T(8,128)S(1)}, f32[1,128,128]{1,2,0:T(8,128)S(1)}, u32[]{:S(2)}, u32[]{:S(2)}) collective-permute-start(f32[1,128,128]{1,2,0:T(8,128)S(1)} %fusion.39), channel_id=1, source_target_pairs={{32,0},{33,1},{34,2},{35,3},{36,4},{37,5},{38,6},{39,7},{40,8},{41... | collective-permute-start | bytes 196616 | tf_op jit(solution)/shard_map/ppermute | solution.py:12
  128.4 5.2 %collective-permute-done.1 = f32[1,128,128]{1,2,0:T(8,128)S(1)} collective-permute-done((f32[1,128,128]{1,2,0:T(8,128)S(1)}, f32[1,128,128]{1,2,0:T(8,128)S(1)}, u32[]{:S(2)}, u32[]{:S(2)}) %collective-permute-start.1) | collective-permute-done | bytes 65568 | tf_op jit(solution)/shard_map/ppermute | solution.py:12
  133.8 11.7 %custom-call.10 = f32[1,128,128]{2,1,0:T(8,128)S(1)} custom-call(f32[1,128,128]{2,1,0:T(8,128)S(1)} %fusion.36), custom_call_target="Cholesky" | custom-call | tf_op jit(solution)/shard_map/vmap(jit(cholesky))/cholesky | solution.py:26
  145.6 0.6 compare_reduce_fusion.1
  146.2 0.7 fusion.26
  146.9 9.8 %custom-call.11 = f32[1,1,128,128]{2,3,1,0:T(8,128)S(1)} custom-call(f32[1,1,128,128]{3,2,1,0:T(8,128)S(1)} %fusion.26), custom_call_target="InvertDiagBlocksLowerTriangular" | custom-call | tf_op jit(solution)/shard_map/vmap(jit(_cho_solve))/triangular_solve | solution.py:27
  156.7 39.4 %all-to-all-done.2 = bf16[192,64,128]{2,0,1:T(8,128)(2,1)S(1)} async-done(((bf16[192,64,128]{2,0,1:T(8,128)(2,1)}), bf16[192,64,128]{2,0,1:T(8,128)(2,1)S(1)}, u32[]{:S(2)}, u32[]{:S(2)}) %all-to-all-start.2) | async-done | bytes 3145760 | tf_op jit(solution)/shard_map/all_to_all | solution.py:49
  196.1 3.0 %fusion.21 = f32[128,128]{0,1:T(8,128)S(1)} fusion(bf16[192,64,128]{2,0,1:T(8,128)(2,1)} %all-to-all-done, bf16[192,64,128]{2,0,1:T(8,128)(2,1)S(1)} %all-to-all-done.2, pred[]{:T(512)S(6)} %and.11), kind=kOutput, calls=%fused_computation.13 | convolution fusion | flops 402685952 | bytes 6356993 | tf_op jit(solution)/shard_map/tgb,tgc->gbc/dot_general | solution.py:56
  199.1 0.3 fusion.34
  199.6 0.3 convolution_subtract_fusion
  200.0 11.7 %custom-call.12 = f32[1,128,128]{2,1,0:T(8,128)S(1)} custom-call(f32[1,128,128]{2,1,0:T(8,128)S(1)} %fusion.29), custom_call_target="Cholesky" | custom-call | tf_op jit(solution)/shard_map/vmap(jit(cholesky))/cholesky | solution.py:26
  211.8 0.6 compare_reduce_fusion
  212.4 0.7 fusion.27
  213.1 9.8 %custom-call.13 = f32[1,1,128,128]{2,3,1,0:T(8,128)S(1)} custom-call(f32[1,1,128,128]{3,2,1,0:T(8,128)S(1)} %fusion.27), custom_call_target="InvertDiagBlocksLowerTriangular" | custom-call | tf_op jit(solution)/shard_map/vmap(jit(_cho_solve))/triangular_solve | solution.py:27
  222.9 0.3 fusion.28
  223.2 0.8 convolution_bitcast_fusion
  224.0 0.7 copy.34
  (15 shorter events, 0.6 us)
Async XLA Ops:
  9.2 13.2 %copy-start = (bf16[192,2,4096]{2,1,0:T(2,128)(2,1)S(1)}, bf16[192,2,4096]{2,1,0:T(2,128)(2,1)}, u32[]{:S(2)}) copy-start(bf16[192,2,4096]{2,1,0:T(2,128)(2,1)} %param.5) | copy-start | bytes 9437188
  9.2 87.5 %all-to-all-start = ((bf16[192,64,128]{2,0,1:T(8,128)(2,1)}), bf16[192,64,128]{2,0,1:T(8,128)(2,1)}, u32[]{:S(2)}, u32[]{:S(2)}) async-start(bf16[192,64,128]{2,0,1:T(8,128)(2,1)} %copy.26), calls=%async_computation | async-start | bytes 6291456 | tf_op jit(solution)/shard_map/all_to_all | solution.py:48
  24.7 83.3 %collective-permute-start = (bf16[192,4096]{1,0:T(8,128)(2,1)S(1)}, bf16[192,4096]{1,0:T(8,128)(2,1)}, u32[]{:S(2)}, u32[]{:S(2)}) collective-permute-start(bf16[192,4096]{1,0:T(8,128)(2,1)S(1)} %get-tuple-element.13), channel_id=1, source_target_pairs={{64,0},{128,64},{192,128},{65,1},{129,65},{193,129},{66,2},{130,66... | collective-permute-start | bytes 4718600 | tf_op jit(solution)/shard_map/ppermute | solution.py:12
  102.5 15.9 %all-to-all-start.1 = ((f32[64,1,2]{2,1,0:T(1,128)}), f32[64,1,2]{2,1,0:T(1,128)S(1)}, u32[]{:S(2)}, u32[]{:S(2)}) async-start(f32[64,1,2]{2,1,0:T(1,128)} %broadcast_in_dim.31), calls=%async_computation.1 | async-start | bytes 65536 | tf_op jit(solution)/shard_map/all_to_all | solution.py:17
  112.0 11.5 %copy-start.1 = (f32[2]{0:T(128)S(1)}, f32[2]{0:T(128)}, u32[]{:S(2)}) copy-start(f32[2]{0:T(128)} %param.6) | copy-start | bytes 28
  118.4 77.8 %all-to-all-start.2 = ((bf16[192,64,128]{2,0,1:T(8,128)(2,1)}), bf16[192,64,128]{2,0,1:T(8,128)(2,1)S(1)}, u32[]{:S(2)}, u32[]{:S(2)}) async-start(bf16[192,64,128]{2,0,1:T(8,128)(2,1)} %copy_bitcast_fusion), calls=%async_computation.2 | async-start | bytes 6291456 | tf_op jit(solution)/shard_map/all_to_all | solution.py:49
  124.8 8.9 %collective-permute-start.1 = (f32[1,128,128]{1,2,0:T(8,128)S(1)}, f32[1,128,128]{1,2,0:T(8,128)S(1)}, u32[]{:S(2)}, u32[]{:S(2)}) collective-permute-start(f32[1,128,128]{1,2,0:T(8,128)S(1)} %fusion.39), channel_id=1, source_target_pairs={{32,0},{33,1},{34,2},{35,3},{36,4},{37,5},{38,6},{39,7},{40,8},{41... | collective-permute-start | bytes 196616 | tf_op jit(solution)/shard_map/ppermute | solution.py:12
where the time goes:
time: 225 us
  waiting for transfers between devices  121 us (54%)
  other arithmetic  51.1 us (23%)
  starting transfers between devices  29.4 us (13%)
  local copies, waits for them, and re-layouts  12.4 us (6%)
  matrix products  9.39 us (4%)
    all_to_all x1, waiting for transfers between devices, local(): lax.all_to_all(sent_pairs[0], 'dp', split_axis=1, concat_axis=0, tiled=True)  70 us
    all_to_all x1, waiting for transfers between devices, local(): lax.all_to_all(sent_pairs[1], 'dp', split_axis=1, concat_axis=0, tiled=True)  39.4 us
    another operation x6, other arithmetic, solve_block(): factor = jnp.linalg.cholesky(system)  24.8 us
    another operation x4, other arithmetic, solve_block(): return jax.scipy.linalg.cho_solve((factor, True), right_side)  20.9 us
    all_to_all x1, starting transfers between devices, local(): lax.all_to_all(sent_pairs[0], 'dp', split_axis=1, concat_axis=0, tiled=True)  13.2 us
    another operation x2, local copies, waits for them, and re-layouts, local(): flattened.reshape(token_rows, group_size, per_device * block_size)  8.53 us
    all_to_all x1, waiting for transfers between devices, sent_to_all(): return lax.all_to_all(copies, axis, split_axis=0, concat_axis=0, tiled=True)  6.34 us
    ppermute x2, starting transfers between devices, passed_along(): return lax.ppermute(block, axis, route)  5.55 us
  transfers between devices with their start and end apart: 5, of which 4 were waited for; matrix products, arithmetic and copies ran while one was open for 16% of the time, Pallas kernels for 0%

commit v1 on v0

v1 whole, which is shorter than its diff:
```python
import functools

import jax
import jax.numpy as jnp
from jax import lax
from jax.experimental import pallas as pl
from jax.experimental.pallas import tpu as pltpu
from jax.sharding import PartitionSpec as P

MESH = pl.DeviceIdType.MESH
HIGHEST = lax.Precision.HIGHEST
B = 128
W = 16
NY, NX, NZ = 4, 2, 8
PIECES = 4
PEERS = ((0, 1), (1, 0), (3, 0), (1, 1), (3, 1), (2, 0), (2, 1))
UNITS = ((0, 0), (1, 0), (0, 1), (2, 0), (1, 1), (3, 0), (2, 1), (3, 1))


def product(a, b):
    return lax.dot_general(
        a, b, (((1,), (0,)), ((), ())), precision=HIGHEST, preferred_element_type=jnp.float32
    )


def product_t(a, b):
    return lax.dot_general(
        a, b, (((1,), (1,)), ((), ())), precision=HIGHEST, preferred_element_type=jnp.float32
    )


def gram(a, b):
    return lax.dot_general(a, b, (((0,), (0,)), ((), ())), preferred_element_type=jnp.float32)


def small_inverse(panel, first):
    row = lax.broadcasted_iota(jnp.int32, (8, B), 0)
    halves = [panel[8 * h : 8 * h + 8] for h in range(W // 8)]
    columns = [
        [jnp.broadcast_to(half[:, first + j : first + j + 1], (8, B)) for half in halves]
        for j in range(W)
    ]
    for j in range(W):
        h, i = divmod(j, 8)
        own = row == i
        pivot = columns[j]
        inverse = 1.0 / pivot[h][i : i + 1]
        for k in range(W):
            if k == j:
                continue
            scaled = columns[k][h][i : i + 1] * inverse
            new = [c - p * scaled for c, p in zip(columns[k], pivot)]
            new[h] = jnp.where(own, scaled, new[h])
            columns[k] = new
        new = [-p * inverse for p in pivot]
        new[h] = jnp.where(own, inverse, new[h])
        columns[j] = new
    return columns


def invert(a):
    lane = lax.broadcasted_iota(jnp.int32, (B, B), 1)
    row = lax.broadcasted_iota(jnp.int32, (W, B), 0)
    for first in range(0, B, W):
        panel = a[first : first + W]
        columns = small_inverse(panel, first)
        inside = (lane >= first) & (lane < first + W)
        identity = (lane[:W] - first == row).astype(jnp.float32)
        rows = jnp.where(inside[:W], identity, panel)
        halves = []
        for h in range(W // 8):
            total = columns[0][h] * rows[0:1]
            for j in range(1, W):
                total = total + columns[j][h] * rows[j : j + 1]
            halves.append(total)
        rows = jnp.concatenate(halves, axis=0)
        rest = jnp.where(inside, 0.0, a) - product(a[:, first : first + W], rows)
        parts = [rest[:first]] if first else []
        parts.append(rows)
        if first + W < B:
            parts.append(rest[first + W :])
        a = jnp.concatenate(parts, axis=0)
    return a


def solve_kernel(diagonal_ref, cross_ref, following_ref, level_ref, inverse_ref, coupling_ref):
    diagonal = lax.broadcasted_iota(jnp.int32, (B, B), 0) == lax.broadcasted_iota(
        jnp.int32, (B, B), 1
    )
    cross = cross_ref[...]
    following = following_ref[...]
    following = jnp.where(diagonal, following + level_ref[1, 0:1, :], following)
    coupling = product(cross, invert(following))
    coupling_ref[0] = coupling
    damped = diagonal_ref[...]
    damped = jnp.where(diagonal, damped + level_ref[0, 0:1, :], damped)
    inverse_ref[0] = invert(damped - product_t(coupling, cross))


def filled(ref, semaphore):
    pltpu.make_async_copy(ref, ref, semaphore).wait()


def gram_kernel(
    tokens,
    x_ref,
    damping_ref,
    diagonal_ref,
    cross_ref,
    following_ref,
    level_ref,
    raw,
    passed,
    partial,
    got,
    reduced,
    follow,
    square,
    square_a,
    square_b,
    square_c,
    level,
    level_next,
    raw_send,
    raw_recv,
    pass_send,
    pass_recv,
    part_send,
    part_recv,
    follow_sem,
    square_send,
    square_recv,
    level_sem,
):
    section, dp = lax.axis_index("section"), lax.axis_index("dp")
    sections = lax.axis_size("section")
    y, x, z = dp // (NX * NZ), (dp // NZ) % NX, dp % NZ
    upper = y // 2
    has_before, has_after = section > 0, section < sections - 1
    before, after = lax.rem(section + sections - 1, sections), lax.rem(section + 1, sections)
    across = lax.rem(y + 2, NY)

    def at(y, x, z):
        return y * (NX * NZ) + x * NZ + z

    def near(dy, dx):
        return lax.rem(y + dy, NY), lax.rem(x + dx, NX)

    def send(src, dst, send_sem, recv_sem, to_section, to_dp):
        return pltpu.make_async_remote_copy(
            src_ref=src,
            dst_ref=dst,
            send_sem=send_sem,
            recv_sem=recv_sem,
            device_id=(to_section, to_dp),
            device_id_type=MESH,
        )

    barrier = pltpu.get_barrier_semaphore()
    greeted = [(section, at(*near(dy, dx), z)) for dy, dx in PEERS]
    for dz in range(1, NZ):
        other = lax.rem(z + dz, NZ)
        greeted += [(section, at(y, x, other)), (section, at(across, x, other))]
    greeted += [(before, dp), (after, dp)]
    greeted += [(jnp.where(upper == 0, before, after), at(across, x, z))]
    for device in greeted:
        pl.semaphore_signal(barrier, inc=1, device_id=device, device_id_type=MESH)
    pl.semaphore_wait(barrier, len(greeted))

    def order(piece):
        return lax.rem(piece + z // 2 + 1, PIECES)

    def source(piece, layer, y, x):
        block = lax.rem(y, 2) * (NX * NZ) + x * NZ + 2 * order(piece) + y // 2
        return x_ref.at[layer, :, pl.ds(pl.multiple_of(block * B, B), B)]

    def start(piece, layer):
        pltpu.make_async_copy(
            source(piece, layer, y, x), raw.at[piece, layer, 0], raw_recv.at[piece, layer]
        ).start()
        for slot, (dy, dx) in enumerate(PEERS, 1):
            to_y, to_x = near(dy, dx)
            send(
                source(piece, layer, to_y, to_x),
                raw.at[piece, layer, slot],
                raw_send,
                raw_recv.at[piece, layer],
                section,
                at(to_y, to_x, z),
            ).start()

    for piece, layer in UNITS[:2]:
        start(piece, layer)

    width = x_ref.shape[2]

    def add_rows(step, totals):
        rows = pl.ds(pl.multiple_of(step * 16, 16), 16)
        out = []
        for layer in range(2):
            total = totals[layer]
            for c in range(width // B):
                value = x_ref[layer, rows, c * B : (c + 1) * B].astype(jnp.float32)
                total = total + value * value
            out.append(total)
        return tuple(out)

    zero = jnp.zeros((16, B), jnp.float32)
    totals = lax.fori_loop(0, x_ref.shape[1] // 16, add_rows, (zero, zero))
    for layer in range(2):
        square[layer] = totals[layer][:8] + totals[layer][8:]
    for slot, (dy, dx) in enumerate(PEERS):
        to_y, to_x = near(dy, dx)
        send(
            square, square_a.at[slot], square_send.at[0], square_recv.at[0], section, at(to_y, to_x, z)
        ).start()
    for piece, layer in UNITS[2:]:
        start(piece, layer)
    filled(square_a, square_recv.at[0])
    total = square[...]
    for slot in range(len(PEERS)):
        total = total + square_a[slot]
    square_c[...] = total
    for dz in range(1, NZ):
        send(
            square_c,
            square_b.at[dz - 1],
            square_send.at[1],
            square_recv.at[1],
            section,
            at(y, x, lax.rem(z + dz, NZ)),
        ).start()

    def target(piece, layer):
        to_y, to_z = lax.rem(y, 2) + 2 * layer, 2 * order(piece) + upper
        return at(to_y, x, to_z), (to_y == y) & (to_z == z)

    def item(piece, layer):
        to_dp, own = target(piece, layer)
        src, dst = partial.at[piece, layer], got.at[z]
        remote = send(src, dst, part_send.at[piece, layer], part_recv, section, to_dp)
        local = pltpu.make_async_copy(src, dst, part_recv)
        return remote, local, own

    def deliver(piece, layer):
        remote, local, own = item(piece, layer)

        @pl.when(own)
        def _():
            local.start()

        @pl.when(jnp.logical_not(own))
        def _():
            remote.start()

    def passing(piece):
        return send(
            raw.at[piece, 0], passed.at[piece], pass_send.at[piece], pass_recv.at[piece], before, dp
        )

    depth = len(PEERS) + 1

    def columns(ref):
        return ref[...].reshape(depth * x_ref.shape[1], B)

    for unit, (piece, layer) in enumerate(UNITS):
        filled(raw.at[piece, layer], raw_recv.at[piece, layer])
        if layer == 0:

            @pl.when(has_before)
            def _():
                passing(piece).start()

        else:
            first, second = columns(raw.at[piece, 0]), columns(raw.at[piece, 1])
            partial[piece, 0, 0] = gram(first, first)
            partial[piece, 0, 1] = gram(first, second)
            deliver(piece, 0)
            partial[piece, 1, 0] = gram(second, second)

            @pl.when(has_after)
            def _():
                filled(passed.at[piece], pass_recv.at[piece])
                partial[piece, 1, 1] = gram(second, columns(passed.at[piece]))

            @pl.when(jnp.logical_not(has_after))
            def _():
                partial[piece, 1, 1] = jnp.zeros((B, B), jnp.float32)

            deliver(piece, 1)
        if unit == 2:
            filled(square_b, square_recv.at[1])
            total = square_c[...]
            for dz in range(1, NZ):
                total = total + square_b[dz - 1]
            for own_layer in range(2):
                trace = jnp.sum(total[own_layer], keepdims=True) * (1.0 / (tokens * width))
                level[own_layer] = jnp.broadcast_to(trace, (8, B)) * damping_ref[own_layer]

            @pl.when(has_before)
            def _():
                send(
                    level.at[0], level_next, level_sem.at[0], level_sem.at[1], before, dp
                ).start()

    filled(got, part_recv)
    for which, out in enumerate((reduced, cross_ref)):
        total = got[0, which]
        for step in range(1, NZ):
            total = total + got[step, which]
        out[...] = total * (1.0 / tokens)
    follows = send(
        reduced,
        follow,
        follow_sem.at[0],
        follow_sem.at[1],
        jnp.where(upper == 0, before, section),
        at(across, x, z),
    )
    first_of_all = jnp.logical_not(has_before) & (upper == 0)
    last_of_all = jnp.logical_not(has_after) & (upper == 1)

    @pl.when(jnp.logical_not(first_of_all))
    def _():
        follows.start()

    diagonal_ref[...] = reduced[...]

    @pl.when(has_after)
    def _():
        filled(level_next, level_sem.at[1])

    @pl.when(upper == 0)
    def _():
        level_ref[0] = level[0]
        level_ref[1] = level[1]

    @pl.when((upper == 1) & has_after)
    def _():
        level_ref[0] = level[1]
        level_ref[1] = level_next[...]

    @pl.when(last_of_all)
    def _():
        level_ref[0] = level[1]
        level_ref[1] = jnp.zeros((8, B), jnp.float32)

    for piece in range(PIECES):
        for layer in range(2):
            remote, _, own = item(piece, layer)
            pl.when(jnp.logical_not(own))(remote.wait_send)
        pl.when(has_before)(passing(piece).wait_send)
    sent = raw.at[:, :, pl.ds(1, len(PEERS))]
    filled(sent, raw_send)
    filled(square_a, square_send.at[0])
    filled(square_b, square_send.at[1])

    @pl.when(has_before)
    def _():
        filled(level_next, level_sem.at[0])

    @pl.when(last_of_all)
    def _():
        following_ref[...] = (
            lax.broadcasted_iota(jnp.int32, (B, B), 0) == lax.broadcasted_iota(jnp.int32, (B, B), 1)
        ).astype(jnp.float32)
        cross_ref[...] = jnp.zeros((B, B), jnp.float32)

    @pl.when(jnp.logical_not(last_of_all))
    def _():
        filled(follow, follow_sem.at[1])
        following_ref[...] = follow[...]

    @pl.when(jnp.logical_not(first_of_all))
    def _():
        filled(follow, follow_sem.at[0])


def local(activations, damping):
    rows, layers, width = activations.shape
    tokens = rows * lax.axis_size("dp")
    by_layer = jnp.transpose(activations, (1, 0, 2))
    depth = len(PEERS) + 1
    f32, bf16 = jnp.float32, jnp.bfloat16
    vmem = pl.BlockSpec(memory_space=pltpu.VMEM)
    block = jax.ShapeDtypeStruct((B, B), f32)
    diagonal, cross, following, level = pl.pallas_call(
        functools.partial(gram_kernel, tokens),
        out_shape=(block, block, block, jax.ShapeDtypeStruct((2, 8, B), f32)),
        in_specs=[vmem, pl.BlockSpec(memory_space=pltpu.SMEM)],
        out_specs=(vmem,) * 4,
        scratch_shapes=[
            pltpu.VMEM((PIECES, 2, depth, rows, B), bf16),
            pltpu.VMEM((PIECES, depth, rows, B), bf16),
            pltpu.VMEM((PIECES, 2, 2, B, B), f32),
            pltpu.VMEM((NZ, 2, B, B), f32),
            pltpu.VMEM((B, B), f32),
            pltpu.VMEM((B, B), f32),
            pltpu.VMEM((2, 8, B), f32),
            pltpu.VMEM((len(PEERS), 2, 8, B), f32),
            pltpu.VMEM((NZ - 1, 2, 8, B), f32),
            pltpu.VMEM((2, 8, B), f32),
            pltpu.VMEM((2, 8, B), f32),
            pltpu.VMEM((8, B), f32),
            pltpu.SemaphoreType.DMA,
            pltpu.SemaphoreType.DMA((PIECES, 2)),
            pltpu.SemaphoreType.DMA((PIECES,)),
            pltpu.SemaphoreType.DMA((PIECES,)),
            pltpu.SemaphoreType.DMA((PIECES, 2)),
            pltpu.SemaphoreType.DMA,
            pltpu.SemaphoreType.DMA((2,)),
            pltpu.SemaphoreType.DMA((2,)),
            pltpu.SemaphoreType.DMA((2,)),
            pltpu.SemaphoreType.DMA((2,)),
        ],
        compiler_params=pltpu.CompilerParams(
            collective_id=0, has_side_effects=True, vmem_limit_bytes=32 * 2**20
        ),
        name="grams",
    )(by_layer, damping)
    result = jax.ShapeDtypeStruct((1, B, B), f32)
    return pl.pallas_call(solve_kernel, out_shape=(result, result), name="solve")(
        diagonal, cross, following, level
    )


def solution(mesh):
    placed = (P("dp", "section", None), P("section"))
    return jax.shard_map(
        local,
        mesh=mesh,
        in_specs=placed,
        out_specs=(P(("section", "dp"), None, None), P(("section", "dp"), None, None)),
        check_vma=False,
    )
```

time: 225 us -> 102 us (0.45)
  the two profiles are of different devices: /device:TPU:4 before, /device:TPU:64 now
where the time goes in v1:
time: 102 us
  Pallas kernels  95 us (93%)
  local copies, waits for them, and re-layouts  6.45 us (6%)
    pallas_call x1, Pallas kernels, local(): pl.pallas_call(functools.partial(gram_kernel, tokens), out_shape=(block,...  84.1 us
    pallas_call x1, Pallas kernels, local(): pl.pallas_call(solve_kernel, out_shape=(result, result), name='solve')  10.9 us
    unnamed x11, local copies, waits for them, and re-layouts  6.45 us

profile of v1, /device:TPU:64, one launch (start us, length us, event | category | flops | bytes accessed | tf_op | source)
XLA Modules:
  0.0 102.1 jit_solution(13946850241207760474)
XLA Ops:
  0.6 0.0 copy-start.4
  0.6 4.0 %copy.6 = bf16[192,2,4096]{2,0,1:T(8,128)(2,1)S(1)} copy(bf16[192,2,4096]{2,1,0:T(2,128)(2,1)} %param.2) | data formatting | bytes 6291456 | tf_op args[0]
  4.6 0.0 copy-done.4
  4.7 84.1 %grams.1 = (f32[128,128]{1,0:T(8,128)S(1)}, f32[128,128]{1,0:T(8,128)S(1)}, f32[128,128]{1,0:T(8,128)S(1)}, f32[2,8,128]{2,1,0:T(8,128)S(1)}) custom-call(bf16[2,192,4096]{2,1,0:T(8,128)(2,1)S(1)} %bitcast.3, f32[2]{0:T(128)S(1)} %copy-done.4), custom_call_target="tpu_custom_call" | custom-call | tf_op jit(solution)/shard_map/grams/pallas_call | solution.py:387
  88.7 0.0 copy-start
  88.7 0.6 copy-done
  89.3 0.0 copy-start.1
  89.3 0.6 copy-done.1
  90.0 0.0 copy-start.2
  90.0 0.6 copy-done.2
  90.6 0.0 copy-start.3
  90.6 0.6 copy-done.3
  91.2 10.9 %solve.1 = (f32[1,128,128]{2,1,0:T(8,128)}, f32[1,128,128]{2,1,0:T(8,128)}) custom-call(f32[128,128]{1,0:T(8,128)} %copy-done, f32[128,128]{1,0:T(8,128)} %copy-done.1, f32[128,128]{1,0:T(8,128)} %copy-done.2, f32[2,8,128]{2,1,0:T(8,128)} %copy-done.3), custom_call_target="tpu_custom_call" | custom-call | tf_op jit(solution)/shard_map/solve/pallas_call | solution.py:422
Async XLA Ops:
  0.6 4.0 %copy-start.4 = (f32[2]{0:T(128)S(1)}, f32[2]{0:T(128)}, u32[]{:S(2)}) copy-start(f32[2]{0:T(128)} %damping_ref.1) | copy-start | bytes 28
  88.7 0.6 copy-start
  89.3 0.6 copy-start.1
  90.0 0.6 copy-start.2
  90.6 0.6 copy-start.3

commit v2 on v1

--- a/solution.py
+++ b/solution.py
@@ -14,6 +14,7 @@
 NY, NX, NZ = 4, 2, 8
 PIECES = 4
 PEERS = ((0, 1), (1, 0), (3, 0), (1, 1), (3, 1), (2, 0), (2, 1))
+AHEAD = 4
 UNITS = ((0, 0), (1, 0), (0, 1), (2, 0), (1, 1), (3, 0), (2, 1), (3, 1))
 
 
@@ -114,6 +115,7 @@
     partial,
     got,
     reduced,
+    moved,
     follow,
     square,
     square_a,
@@ -127,6 +129,7 @@
     pass_recv,
     part_send,
     part_recv,
+    move_sem,
     follow_sem,
     square_send,
     square_recv,
@@ -139,6 +142,8 @@
     has_before, has_after = section > 0, section < sections - 1
     before, after = lax.rem(section + sections - 1, sections), lax.rem(section + 1, sections)
     across = lax.rem(y + 2, NY)
+    beside = z + 1 - 2 * lax.rem(z, 2)
+    keeps = lax.rem(z, 2) == upper
 
     def at(y, x, z):
         return y * (NX * NZ) + x * NZ + z
@@ -160,9 +165,10 @@
     greeted = [(section, at(*near(dy, dx), z)) for dy, dx in PEERS]
     for dz in range(1, NZ):
         other = lax.rem(z + dz, NZ)
-        greeted += [(section, at(y, x, other)), (section, at(across, x, other))]
-    greeted += [(before, dp), (after, dp)]
-    greeted += [(jnp.where(upper == 0, before, after), at(across, x, z))]
+        greeted += [(section, at(y, x, other))]
+    greeted += [(before, dp), (after, dp), (section, at(across, x, beside))]
+    greeted += [(before, at(other_y, x, other_z)) for other_y, other_z in ((across, z), (y, beside))]
+    greeted += [(after, at(other_y, x, other_z)) for other_y, other_z in ((across, z), (y, beside))]
     for device in greeted:
         pl.semaphore_signal(barrier, inc=1, device_id=device, device_id_type=MESH)
     pl.semaphore_wait(barrier, len(greeted))
@@ -214,7 +220,7 @@
         send(
             square, square_a.at[slot], square_send.at[0], square_recv.at[0], section, at(to_y, to_x, z)
         ).start()
-    for piece, layer in UNITS[2:]:
+    for piece, layer in UNITS[2:AHEAD]:
         start(piece, layer)
     filled(square_a, square_recv.at[0])
     total = square[...]
@@ -232,8 +238,8 @@
         ).start()
 
     def target(piece, layer):
-        to_y, to_z = lax.rem(y, 2) + 2 * layer, 2 * order(piece) + upper
-        return at(to_y, x, to_z), (to_y == y) & (to_z == z)
+        to_z = 2 * order(piece) + layer
+        return at(y, x, to_z), to_z == z
 
     def item(piece, layer):
         to_dp, own = target(piece, layer)
@@ -288,6 +294,8 @@
                 partial[piece, 1, 1] = jnp.zeros((B, B), jnp.float32)
 
             deliver(piece, 1)
+        if unit + AHEAD < len(UNITS):
+            start(*UNITS[unit + AHEAD])
         if unit == 2:
             filled(square_b, square_recv.at[1])
             total = square_c[...]
@@ -304,27 +312,33 @@
                 ).start()
 
     filled(got, part_recv)
-    for which, out in enumerate((reduced, cross_ref)):
+    for which in range(2):
         total = got[0, which]
         for step in range(1, NZ):
             total = total + got[step, which]
-        out[...] = total * (1.0 / tokens)
+        reduced[which] = total * (1.0 / tokens)
+    layer_here = jnp.where(keeps, upper, 1 - upper)
+    moves = send(
+        reduced, moved, move_sem.at[0], move_sem.at[1], section, at(across, x, beside)
+    )
     follows = send(
-        reduced,
+        reduced.at[0],
         follow,
         follow_sem.at[0],
         follow_sem.at[1],
-        jnp.where(upper == 0, before, section),
-        at(across, x, z),
-    )
-    first_of_all = jnp.logical_not(has_before) & (upper == 0)
+        jnp.where(layer_here == 0, before, section),
+        at(jnp.where(keeps, across, y), x, jnp.where(keeps, z, beside)),
+    )
+    first_of_all = jnp.logical_not(has_before) & (layer_here == 0)
     last_of_all = jnp.logical_not(has_after) & (upper == 1)
 
     @pl.when(jnp.logical_not(first_of_all))
     def _():
         follows.start()
 
-    diagonal_ref[...] = reduced[...]
+    @pl.when(jnp.logical_not(keeps))
+    def _():
+        moves.start()
 
     @pl.when(has_after)
     def _():
@@ -359,6 +373,17 @@
     def _():
         filled(level_next, level_sem.at[0])
 
+    @pl.when(keeps)
+    def _():
+        diagonal_ref[...] = reduced[0]
+        cross_ref[...] = reduced[1]
+
+    @pl.when(jnp.logical_not(keeps))
+    def _():
+        filled(moved, move_sem.at[1])
+        diagonal_ref[...] = moved[0]
+        cross_ref[...] = moved[1]
+
     @pl.when(last_of_all)
     def _():
         following_ref[...] = (
@@ -370,6 +395,10 @@
     def _():
         filled(follow, follow_sem.at[1])
         following_ref[...] = follow[...]
+
+    @pl.when(jnp.logical_not(keeps))
+    def _():
+        filled(moved, move_sem.at[0])
 
     @pl.when(jnp.logical_not(first_of_all))
     def _():
@@ -394,7 +423,8 @@
             pltpu.VMEM((PIECES, depth, rows, B), bf16),
             pltpu.VMEM((PIECES, 2, 2, B, B), f32),
             pltpu.VMEM((NZ, 2, B, B), f32),
-            pltpu.VMEM((B, B), f32),
+            pltpu.VMEM((2, B, B), f32),
+            pltpu.VMEM((2, B, B), f32),
             pltpu.VMEM((B, B), f32),
             pltpu.VMEM((2, 8, B), f32),
             pltpu.VMEM((len(PEERS), 2, 8, B), f32),
@@ -412,6 +442,7 @@
             pltpu.SemaphoreType.DMA((2,)),
             pltpu.SemaphoreType.DMA((2,)),
             pltpu.SemaphoreType.DMA((2,)),
+            pltpu.SemaphoreType.DMA((2,)),
         ],
         compiler_params=pltpu.CompilerParams(
             collective_id=0, has_side_effects=True, vmem_limit_bytes=32 * 2**20
@@ -419,9 +450,13 @@
         name="grams",
     )(by_layer, damping)
     result = jax.ShapeDtypeStruct((1, B, B), f32)
-    return pl.pallas_call(solve_kernel, out_shape=(result, result), name="solve")(
-        diagonal, cross, following, level
-    )
+    return pl.pallas_call(
+        solve_kernel,
+        out_shape=(result, result),
+        in_specs=[vmem] * 4,
+        compiler_params=pltpu.CompilerParams(vmem_limit_bytes=8 * 2**20),
+        name="solve",
+    )(diagonal, cross, following, level)
 
 
 def solution(mesh):

time: 102 us -> 86.7 us (0.85)
  the two profiles are of different devices: /device:TPU:64 before, /device:TPU:17 now
where the time goes in v2:
time: 86.7 us; the launch traced here: 85.6 us
  Pallas kernels  81 us (93%)
  local copies, waits for them, and re-layouts  4.01 us (5%)
    pallas_call x1, Pallas kernels, local(): pl.pallas_call(functools.partial(gram_kernel, tokens), out_shape=(block,...  71 us
    pallas_call x1, Pallas kernels, local(): pl.pallas_call(solve_kernel, out_shape=(result, result), in_specs=[vmem]...  10 us
    unnamed x3, local copies, waits for them, and re-layouts  4.01 us

profile of v2, /device:TPU:17, one launch (start us, length us, event | category | flops | bytes accessed | tf_op | source)
XLA Modules:
  0.0 85.6 jit_solution(11000740471319229776)
XLA Ops:
  0.6 0.0 copy-start
  0.6 4.0 %copy.6 = bf16[192,2,4096]{2,0,1:T(8,128)(2,1)S(1)} copy(bf16[192,2,4096]{2,1,0:T(2,128)(2,1)} %param.2) | data formatting | bytes 6291456 | tf_op args[0]
  4.6 0.0 copy-done
  4.7 71.0 %grams.1 = (f32[128,128]{1,0:T(8,128)S(1)}, f32[128,128]{1,0:T(8,128)S(1)}, f32[128,128]{1,0:T(8,128)S(1)}, f32[2,8,128]{2,1,0:T(8,128)S(1)}) custom-call(bf16[2,192,4096]{2,1,0:T(8,128)(2,1)S(1)} %bitcast.3, f32[2]{0:T(128)S(1)} %copy-done), custom_call_target="tpu_custom_call" | custom-call | tf_op jit(solution)/shard_map/grams/pallas_call | solution.py:416
  75.6 10.0 %solve.1 = (f32[1,128,128]{2,1,0:T(8,128)}, f32[1,128,128]{2,1,0:T(8,128)}) custom-call(f32[128,128]{1,0:T(8,128)S(1)} %get-tuple-element.6.diagonal_ref, f32[128,128]{1,0:T(8,128)S(1)} %get-tuple-element.7.cross_ref, f32[128,128]{1,0:T(8,128)S(1)} %get-tuple-element.8.following_ref, f32[2,8,128]{2,1,0:T(8,128)S(1)} %get-tuple-element.9.level_ref), custom_call_target="tpu_custom_call" | custom-call | tf_op jit(solution)/shard_map/solve/pallas_call | solution.py:453
Async XLA Ops:
  0.6 4.0 %copy-start = (f32[2]{0:T(128)S(1)}, f32[2]{0:T(128)}, u32[]{:S(2)}) copy-start(f32[2]{0:T(128)} %damping_ref.1) | copy-start | bytes 28

commit v3 on v2

--- a/solution.py
+++ b/solution.py
@@ -14,8 +14,11 @@
 NY, NX, NZ = 4, 2, 8
 PIECES = 4
 PEERS = ((0, 1), (1, 0), (3, 0), (1, 1), (3, 1), (2, 0), (2, 1))
+TURN = (2, 1, 3, 0)
+LENT = (0, 2)
+LATER = 3
 AHEAD = 4
-UNITS = ((0, 0), (1, 0), (0, 1), (2, 0), (1, 1), (3, 0), (2, 1), (3, 1))
+UNITS = tuple((piece, layer) for piece in range(PIECES) for layer in range(2))
 
 
 def product(a, b):
@@ -62,24 +65,35 @@
 def invert(a):
     lane = lax.broadcasted_iota(jnp.int32, (B, B), 1)
     row = lax.broadcasted_iota(jnp.int32, (W, B), 0)
+    panel = a[:W]
     for first in range(0, B, W):
-        panel = a[first : first + W]
+        last = first + W
         columns = small_inverse(panel, first)
-        inside = (lane >= first) & (lane < first + W)
+        inside = (lane >= first) & (lane < last)
         identity = (lane[:W] - first == row).astype(jnp.float32)
-        rows = jnp.where(inside[:W], identity, panel)
+        panel = jnp.where(inside[:W], identity, panel)
         halves = []
         for h in range(W // 8):
-            total = columns[0][h] * rows[0:1]
+            total = columns[0][h] * panel[0:1]
             for j in range(1, W):
-                total = total + columns[j][h] * rows[j : j + 1]
+                total = total + columns[j][h] * panel[j : j + 1]
             halves.append(total)
         rows = jnp.concatenate(halves, axis=0)
-        rest = jnp.where(inside, 0.0, a) - product(a[:, first : first + W], rows)
+        halves = []
+        for h in range(W // 8 if last < B else 0):
+            below = a[last + 8 * h : last + 8 * h + 8]
+            total = jnp.where(inside[:8], 0.0, below)
+            for j in range(W):
+                factor = jnp.broadcast_to(below[:, first + j : first + j + 1], (8, B))
+                total = total - factor * rows[j : j + 1]
+            halves.append(total)
+        if halves:
+            panel = jnp.concatenate(halves, axis=0)
+        rest = jnp.where(inside, 0.0, a) - product(a[:, first:last], rows)
         parts = [rest[:first]] if first else []
         parts.append(rows)
-        if first + W < B:
-            parts.append(rest[first + W :])
+        if last < B:
+            parts.append(rest[last:])
         a = jnp.concatenate(parts, axis=0)
     return a
 
@@ -104,15 +118,19 @@
 
 def gram_kernel(
     tokens,
-    x_ref,
+    x_hbm,
     damping_ref,
     diagonal_ref,
     cross_ref,
     following_ref,
     level_ref,
+    mixed,
+    x_ref,
     raw,
     passed,
+    lent,
     partial,
+    returned,
     got,
     reduced,
     moved,
@@ -123,10 +141,14 @@
     square_c,
     level,
     level_next,
+    load_sem,
     raw_send,
     raw_recv,
     pass_send,
     pass_recv,
+    lend_send,
+    lend_recv,
+    return_send,
     part_send,
     part_recv,
     move_sem,
@@ -140,6 +162,7 @@
     y, x, z = dp // (NX * NZ), (dp // NZ) % NX, dp % NZ
     upper = y // 2
     has_before, has_after = section > 0, section < sections - 1
+    lends, borrows = section == sections // 2 - 1, section == sections // 2
     before, after = lax.rem(section + sections - 1, sections), lax.rem(section + 1, sections)
     across = lax.rem(y + 2, NY)
     beside = z + 1 - 2 * lax.rem(z, 2)
@@ -161,24 +184,51 @@
             device_id_type=MESH,
         )
 
+    load = pltpu.make_async_copy(x_hbm, mixed, load_sem)
+    load.start()
     barrier = pltpu.get_barrier_semaphore()
     greeted = [(section, at(*near(dy, dx), z)) for dy, dx in PEERS]
     for dz in range(1, NZ):
         other = lax.rem(z + dz, NZ)
-        greeted += [(section, at(y, x, other))]
+        greeted += [(to_section, at(y, x, other)) for to_section in (before, section, after)]
     greeted += [(before, dp), (after, dp), (section, at(across, x, beside))]
-    greeted += [(before, at(other_y, x, other_z)) for other_y, other_z in ((across, z), (y, beside))]
-    greeted += [(after, at(other_y, x, other_z)) for other_y, other_z in ((across, z), (y, beside))]
+    greeted += [(before, at(across, x, z)), (after, at(across, x, z))]
     for device in greeted:
         pl.semaphore_signal(barrier, inc=1, device_id=device, device_id_type=MESH)
-    pl.semaphore_wait(barrier, len(greeted))
-
     def order(piece):
-        return lax.rem(piece + z // 2 + 1, PIECES)
+        return lax.rem(z // 2 + TURN[piece], PIECES)
+
+    def block_of(piece, y, x):
+        return (y % 2) * (NX * NZ) + x * NZ + y // 2 + 2 * order(piece)
 
     def source(piece, layer, y, x):
-        block = lax.rem(y, 2) * (NX * NZ) + x * NZ + 2 * order(piece) + y // 2
-        return x_ref.at[layer, :, pl.ds(pl.multiple_of(block * B, B), B)]
+        return x_ref.at[layer, block_of(piece, y, x)]
+
+    rows, layers, width = mixed.shape
+    part = rows // 2
+    picked = lax.broadcasted_iota(jnp.int32, (layers * part, layers * part), 0)
+    place = lax.broadcasted_iota(jnp.int32, (layers * part, layers * part), 1)
+    picked = layers * (picked % part) + picked // part == place
+    picked = picked.astype(jnp.bfloat16)
+
+    def by_layer(piece):
+        blocks = [block_of(piece, y, x) for y in range(NY) for x in range(NX)]
+        for top in range(0, rows, part):
+            both = jnp.concatenate(
+                [
+                    mixed[top : top + part, :, pl.ds(pl.multiple_of(block * B, B), B)]
+                    for block in blocks
+                ],
+                axis=2,
+            ).reshape(layers * part, len(blocks) * B)
+            apart = lax.dot_general(
+                picked, both, (((1,), (0,)), ((), ())), preferred_element_type=jnp.float32
+            ).astype(jnp.bfloat16)
+            for layer in range(layers):
+                for i, block in enumerate(blocks):
+                    x_ref[layer, block, top : top + part, :] = apart[
+                        layer * part : (layer + 1) * part, i * B : (i + 1) * B
+                    ]
 
     def start(piece, layer):
         pltpu.make_async_copy(
@@ -195,24 +245,28 @@
                 at(to_y, to_x, z),
             ).start()
 
-    for piece, layer in UNITS[:2]:
-        start(piece, layer)
-
-    width = x_ref.shape[2]
-
-    def add_rows(step, totals):
-        rows = pl.ds(pl.multiple_of(step * 16, 16), 16)
+    load.wait()
+    by_layer(0)
+    pl.semaphore_wait(barrier, len(greeted))
+    start(*UNITS[0])
+    by_layer(1)
+    start(*UNITS[1])
+    start(*UNITS[2])
+    by_layer(2)
+    by_layer(3)
+
+    def add_block(block, totals):
         out = []
         for layer in range(2):
             total = totals[layer]
-            for c in range(width // B):
-                value = x_ref[layer, rows, c * B : (c + 1) * B].astype(jnp.float32)
+            for top in range(0, rows, 16):
+                value = x_ref[layer, block, top : top + 16, :].astype(jnp.float32)
                 total = total + value * value
             out.append(total)
         return tuple(out)
 
     zero = jnp.zeros((16, B), jnp.float32)
-    totals = lax.fori_loop(0, x_ref.shape[1] // 16, add_rows, (zero, zero))
+    totals = lax.fori_loop(0, width // B, add_block, (zero, zero))
     for layer in range(2):
         square[layer] = totals[layer][:8] + totals[layer][8:]
     for slot, (dy, dx) in enumerate(PEERS):
@@ -220,7 +274,7 @@
         send(
             square, square_a.at[slot], square_send.at[0], square_recv.at[0], section, at(to_y, to_x, z)
         ).start()
-    for piece, layer in UNITS[2:AHEAD]:
+    for piece, layer in UNITS[3:AHEAD]:
         start(piece, layer)
     filled(square_a, square_recv.at[0])
     total = square[...]
@@ -241,15 +295,15 @@
         to_z = 2 * order(piece) + layer
         return at(y, x, to_z), to_z == z
 
-    def item(piece, layer):
+    def item(piece, layer, which):
         to_dp, own = target(piece, layer)
-        src, dst = partial.at[piece, layer], got.at[z]
-        remote = send(src, dst, part_send.at[piece, layer], part_recv, section, to_dp)
+        src, dst = partial.at[piece, layer, which], got.at[z, which]
+        remote = send(src, dst, part_send.at[piece, layer, which], part_recv, section, to_dp)
         local = pltpu.make_async_copy(src, dst, part_recv)
         return remote, local, own
 
-    def deliver(piece, layer):
-        remote, local, own = item(piece, layer)
+    def deliver(piece, layer, which):
+        remote, local, own = item(piece, layer, which)
 
         @pl.when(own)
         def _():
@@ -264,36 +318,69 @@
             raw.at[piece, 0], passed.at[piece], pass_send.at[piece], pass_recv.at[piece], before, dp
         )
 
+    def lending(piece):
+        slot = LENT.index(piece)
+        return send(
+            raw.at[piece, 1], lent.at[slot], lend_send.at[slot], lend_recv.at[slot], after, dp
+        )
+
+    def returning(piece):
+        slot = LENT.index(piece)
+        return send(
+            returned.at[slot],
+            got.at[z, 1],
+            return_send.at[slot],
+            part_recv,
+            before,
+            target(piece, 1)[0],
+        )
+
+    def passes(piece):
+        return has_before & jnp.logical_not(borrows) if piece in LENT else has_before
+
+    def receives(piece):
+        return has_after & jnp.logical_not(lends) if piece in LENT else has_after
+
     depth = len(PEERS) + 1
 
     def columns(ref):
-        return ref[...].reshape(depth * x_ref.shape[1], B)
+        return ref[...].reshape(depth * rows, B)
 
     for unit, (piece, layer) in enumerate(UNITS):
         filled(raw.at[piece, layer], raw_recv.at[piece, layer])
         if layer == 0:
-
-            @pl.when(has_before)
-            def _():
-                passing(piece).start()
-
+            pl.when(passes(piece))(passing(piece).start)
         else:
+            if piece in LENT:
+                pl.when(lends)(lending(piece).start)
             first, second = columns(raw.at[piece, 0]), columns(raw.at[piece, 1])
             partial[piece, 0, 0] = gram(first, first)
+            deliver(piece, 0, 0)
             partial[piece, 0, 1] = gram(first, second)
-            deliver(piece, 0)
+            deliver(piece, 0, 1)
             partial[piece, 1, 0] = gram(second, second)
-
-            @pl.when(has_after)
+            deliver(piece, 1, 0)
+
+            @pl.when(receives(piece))
             def _():
                 filled(passed.at[piece], pass_recv.at[piece])
                 partial[piece, 1, 1] = gram(second, columns(passed.at[piece]))
+                deliver(piece, 1, 1)
 
             @pl.when(jnp.logical_not(has_after))
             def _():
                 partial[piece, 1, 1] = jnp.zeros((B, B), jnp.float32)
-
-            deliver(piece, 1)
+                deliver(piece, 1, 1)
+
+        for slot, borrowed in enumerate(LENT):
+            if unit == 2 * borrowed + LATER:
+
+                @pl.when(borrows)
+                def _():
+                    filled(lent.at[slot], lend_recv.at[slot])
+                    returned[slot] = gram(columns(lent.at[slot]), columns(raw.at[borrowed, 0]))
+                    returning(borrowed).start()
+
         if unit + AHEAD < len(UNITS):
             start(*UNITS[unit + AHEAD])
         if unit == 2:
@@ -361,9 +448,16 @@
 
     for piece in range(PIECES):
         for layer in range(2):
-            remote, _, own = item(piece, layer)
-            pl.when(jnp.logical_not(own))(remote.wait_send)
-        pl.when(has_before)(passing(piece).wait_send)
+            for which in range(2):
+                remote, _, own = item(piece, layer, which)
+                started = jnp.logical_not(own)
+                if (layer, which) == (1, 1) and piece in LENT:
+                    started = started & jnp.logical_not(lends)
+                pl.when(started)(remote.wait_send)
+        pl.when(passes(piece))(passing(piece).wait_send)
+    for piece in LENT:
+        pl.when(lends)(lending(piece).wait_send)
+        pl.when(borrows)(returning(piece).wait_send)
     sent = raw.at[:, :, pl.ds(1, len(PEERS))]
     filled(sent, raw_send)
     filled(square_a, square_send.at[0])
@@ -408,7 +502,6 @@
 def local(activations, damping):
     rows, layers, width = activations.shape
     tokens = rows * lax.axis_size("dp")
-    by_layer = jnp.transpose(activations, (1, 0, 2))
     depth = len(PEERS) + 1
     f32, bf16 = jnp.float32, jnp.bfloat16
     vmem = pl.BlockSpec(memory_space=pltpu.VMEM)
@@ -416,12 +509,16 @@
     diagonal, cross, following, level = pl.pallas_call(
         functools.partial(gram_kernel, tokens),
         out_shape=(block, block, block, jax.ShapeDtypeStruct((2, 8, B), f32)),
-        in_specs=[vmem, pl.BlockSpec(memory_space=pltpu.SMEM)],
+        in_specs=[pl.BlockSpec(memory_space=pl.ANY), pl.BlockSpec(memory_space=pltpu.SMEM)],
         out_specs=(vmem,) * 4,
         scratch_shapes=[
+            pltpu.VMEM((rows, layers, width), bf16),
+            pltpu.VMEM((layers, width // B, rows, B), bf16),
             pltpu.VMEM((PIECES, 2, depth, rows, B), bf16),
             pltpu.VMEM((PIECES, depth, rows, B), bf16),
+            pltpu.VMEM((len(LENT), depth, rows, B), bf16),
             pltpu.VMEM((PIECES, 2, 2, B, B), f32),
+            pltpu.VMEM((len(LENT), B, B), f32),
             pltpu.VMEM((NZ, 2, B, B), f32),
             pltpu.VMEM((2, B, B), f32),
             pltpu.VMEM((2, B, B), f32),
@@ -433,10 +530,14 @@
             pltpu.VMEM((2, 8, B), f32),
             pltpu.VMEM((8, B), f32),
             pltpu.SemaphoreType.DMA,
+            pltpu.SemaphoreType.DMA,
             pltpu.SemaphoreType.DMA((PIECES, 2)),
             pltpu.SemaphoreType.DMA((PIECES,)),
             pltpu.SemaphoreType.DMA((PIECES,)),
-            pltpu.SemaphoreType.DMA((PIECES, 2)),
+            pltpu.SemaphoreType.DMA((len(LENT),)),
+            pltpu.SemaphoreType.DMA((len(LENT),)),
+            pltpu.SemaphoreType.DMA((len(LENT),)),
+            pltpu.SemaphoreType.DMA((PIECES, 2, 2)),
             pltpu.SemaphoreType.DMA,
             pltpu.SemaphoreType.DMA((2,)),
             pltpu.SemaphoreType.DMA((2,)),
@@ -445,16 +546,14 @@
             pltpu.SemaphoreType.DMA((2,)),
         ],
         compiler_params=pltpu.CompilerParams(
-            collective_id=0, has_side_effects=True, vmem_limit_bytes=32 * 2**20
+            collective_id=0, has_side_effects=True, vmem_limit_bytes=123 * 2**19
         ),
         name="grams",
-    )(by_layer, damping)
+    )(activations, damping)
     result = jax.ShapeDtypeStruct((1, B, B), f32)
     return pl.pallas_call(
         solve_kernel,
         out_shape=(result, result),
-        in_specs=[vmem] * 4,
-        compiler_params=pltpu.CompilerParams(vmem_limit_bytes=8 * 2**20),
         name="solve",
     )(diagonal, cross, following, level)
 

time: 86.7 us -> 78.8 us (0.909); the launches traced: 85.6 us -> 78.7 us
  local copies, waits for them, and re-layouts: 4.01 us -> 0 us
  Pallas kernels: 81 us -> 78 us
    unnamed x3 -> x0, local copies, waits for them, and re-layouts: 4.01 us -> none
    pallas_call x1, Pallas kernels: 71 us -> 69.1 us  [local(): pl.pallas_call(functools.partial(gram_kernel, tokens), out_shape=(block,...]
    pallas_call x1, Pallas kernels: 10 us -> 8.96 us  [local(): pl.pallas_call(solve_kernel, out_shape=(result, result), name='solve')]
where the time goes in v3:
time: 78.8 us; the launch traced here: 78.7 us
  Pallas kernels  78 us (99%)
    pallas_call x1, Pallas kernels, local(): pl.pallas_call(functools.partial(gram_kernel, tokens), out_shape=(block,...  69.1 us
    pallas_call x1, Pallas kernels, local(): pl.pallas_call(solve_kernel, out_shape=(result, result), name='solve')  8.96 us

profile of v3, /device:TPU:17, one launch (start us, length us, event | category | flops | bytes accessed | tf_op | source)
XLA Modules:
  0.0 78.7 jit_solution(13638147995987425030)
XLA Ops:
  0.6 69.1 %grams.1 = (f32[128,128]{1,0:T(8,128)}, f32[128,128]{1,0:T(8,128)}, f32[128,128]{1,0:T(8,128)}, f32[2,8,128]{2,1,0:T(8,128)}) custom-call(bf16[192,2,4096]{2,1,0:T(2,128)(2,1)} %x_hbm.1, f32[2]{0:T(128)} %damping_ref.1), custom_call_target="tpu_custom_call" | custom-call | tf_op jit(solution)/shard_map/grams/pallas_call | solution.py:509
  69.7 9.0 %solve.1 = (f32[1,128,128]{2,1,0:T(8,128)}, f32[1,128,128]{2,1,0:T(8,128)}) custom-call(f32[128,128]{1,0:T(8,128)} %get-tuple-element.6.diagonal_ref, f32[128,128]{1,0:T(8,128)} %get-tuple-element.7.cross_ref, f32[128,128]{1,0:T(8,128)} %get-tuple-element.8.following_ref, f32[2,8,128]{2,1,0:T(8,128)} %get-tuple-element.9.level_ref), custom_call_target="tpu_custom_call" | custom-call | tf_op jit(solution)/shard_map/solve/pallas_call | solution.py:554

commit v4 on v3

--- a/solution.py
+++ b/solution.py
@@ -17,6 +17,7 @@
 TURN = (2, 1, 3, 0)
 LENT = (0, 2)
 LATER = 3
+SQUARES = (2, 4)
 AHEAD = 4
 UNITS = tuple((piece, layer) for piece in range(PIECES) for layer in range(2))
 
@@ -276,20 +277,6 @@
         ).start()
     for piece, layer in UNITS[3:AHEAD]:
         start(piece, layer)
-    filled(square_a, square_recv.at[0])
-    total = square[...]
-    for slot in range(len(PEERS)):
-        total = total + square_a[slot]
-    square_c[...] = total
-    for dz in range(1, NZ):
-        send(
-            square_c,
-            square_b.at[dz - 1],
-            square_send.at[1],
-            square_recv.at[1],
-            section,
-            at(y, x, lax.rem(z + dz, NZ)),
-        ).start()
 
     def target(piece, layer):
         to_z = 2 * order(piece) + layer
@@ -297,9 +284,9 @@
 
     def item(piece, layer, which):
         to_dp, own = target(piece, layer)
-        src, dst = partial.at[piece, layer, which], got.at[z, which]
-        remote = send(src, dst, part_send.at[piece, layer, which], part_recv, section, to_dp)
-        local = pltpu.make_async_copy(src, dst, part_recv)
+        src, dst = partial.at[piece, layer, which], got.at[which, z]
+        remote = send(src, dst, part_send.at[piece, layer, which], part_recv.at[which], section, to_dp)
+        local = pltpu.make_async_copy(src, dst, part_recv.at[which])
         return remote, local, own
 
     def deliver(piece, layer, which):
@@ -328,9 +315,9 @@
         slot = LENT.index(piece)
         return send(
             returned.at[slot],
-            got.at[z, 1],
+            got.at[1, z],
             return_send.at[slot],
-            part_recv,
+            part_recv.at[1],
             before,
             target(piece, 1)[0],
         )
@@ -350,16 +337,17 @@
         filled(raw.at[piece, layer], raw_recv.at[piece, layer])
         if layer == 0:
             pl.when(passes(piece))(passing(piece).start)
+            first = columns(raw.at[piece, 0])
+            partial[piece, 0, 0] = gram(first, first)
+            deliver(piece, 0, 0)
         else:
             if piece in LENT:
                 pl.when(lends)(lending(piece).start)
             first, second = columns(raw.at[piece, 0]), columns(raw.at[piece, 1])
-            partial[piece, 0, 0] = gram(first, first)
-            deliver(piece, 0, 0)
+            partial[piece, 1, 0] = gram(second, second)
+            deliver(piece, 1, 0)
             partial[piece, 0, 1] = gram(first, second)
             deliver(piece, 0, 1)
-            partial[piece, 1, 0] = gram(second, second)
-            deliver(piece, 1, 0)
 
             @pl.when(receives(piece))
             def _():
@@ -383,7 +371,22 @@
 
         if unit + AHEAD < len(UNITS):
             start(*UNITS[unit + AHEAD])
-        if unit == 2:
+        if unit == SQUARES[0]:
+            filled(square_a, square_recv.at[0])
+            total = square[...]
+            for slot in range(len(PEERS)):
+                total = total + square_a[slot]
+            square_c[...] = total
+            for dz in range(1, NZ):
+                send(
+                    square_c,
+                    square_b.at[dz - 1],
+                    square_send.at[1],
+                    square_recv.at[1],
+                    section,
+                    at(y, x, lax.rem(z + dz, NZ)),
+                ).start()
+        if unit == SQUARES[1]:
             filled(square_b, square_recv.at[1])
             total = square_c[...]
             for dz in range(1, NZ):
@@ -398,16 +401,18 @@
                     level.at[0], level_next, level_sem.at[0], level_sem.at[1], before, dp
                 ).start()
 
-    filled(got, part_recv)
-    for which in range(2):
-        total = got[0, which]
-        for step in range(1, NZ):
-            total = total + got[step, which]
-        reduced[which] = total * (1.0 / tokens)
     layer_here = jnp.where(keeps, upper, 1 - upper)
-    moves = send(
-        reduced, moved, move_sem.at[0], move_sem.at[1], section, at(across, x, beside)
-    )
+    moves = [
+        send(
+            reduced.at[which],
+            moved.at[which],
+            move_sem.at[0, which],
+            move_sem.at[1, which],
+            section,
+            at(across, x, beside),
+        )
+        for which in range(2)
+    ]
     follows = send(
         reduced.at[0],
         follow,
@@ -419,13 +424,15 @@
     first_of_all = jnp.logical_not(has_before) & (layer_here == 0)
     last_of_all = jnp.logical_not(has_after) & (upper == 1)
 
-    @pl.when(jnp.logical_not(first_of_all))
-    def _():
-        follows.start()
-
-    @pl.when(jnp.logical_not(keeps))
-    def _():
-        moves.start()
+    for which in range(2):
+        filled(got.at[which], part_recv.at[which])
+        total = got[which, 0]
+        for step in range(1, NZ):
+            total = total + got[which, step]
+        reduced[which] = total * (1.0 / tokens)
+        if which == 0:
+            pl.when(jnp.logical_not(first_of_all))(follows.start)
+        pl.when(jnp.logical_not(keeps))(moves[which].start)
 
     @pl.when(has_after)
     def _():
@@ -474,7 +481,8 @@
 
     @pl.when(jnp.logical_not(keeps))
     def _():
-        filled(moved, move_sem.at[1])
+        for which in range(2):
+            filled(moved.at[which], move_sem.at[1, which])
         diagonal_ref[...] = moved[0]
         cross_ref[...] = moved[1]
 
@@ -492,7 +500,8 @@
 
     @pl.when(jnp.logical_not(keeps))
     def _():
-        filled(moved, move_sem.at[0])
+        for which in range(2):
+            filled(moved.at[which], move_sem.at[0, which])
 
     @pl.when(jnp.logical_not(first_of_all))
     def _():
@@ -519,7 +528,7 @@
             pltpu.VMEM((len(LENT), depth, rows, B), bf16),
             pltpu.VMEM((PIECES, 2, 2, B, B), f32),
             pltpu.VMEM((len(LENT), B, B), f32),
-            pltpu.VMEM((NZ, 2, B, B), f32),
+            pltpu.VMEM((2, NZ, B, B), f32),
             pltpu.VMEM((2, B, B), f32),
             pltpu.VMEM((2, B, B), f32),
             pltpu.VMEM((B, B), f32),
@@ -538,8 +547,8 @@
             pltpu.SemaphoreType.DMA((len(LENT),)),
             pltpu.SemaphoreType.DMA((len(LENT),)),
             pltpu.SemaphoreType.DMA((PIECES, 2, 2)),
-            pltpu.SemaphoreType.DMA,
             pltpu.SemaphoreType.DMA((2,)),
+            pltpu.SemaphoreType.DMA((2, 2)),
             pltpu.SemaphoreType.DMA((2,)),
             pltpu.SemaphoreType.DMA((2,)),
             pltpu.SemaphoreType.DMA((2,)),

time: 78.8 us -> 76.5 us (0.971)
  Pallas kernels: 78 us -> 75.7 us
    pallas_call x1, Pallas kernels: 69.1 us -> 66.7 us  [local(): pl.pallas_call(functools.partial(gram_kernel, tokens), out_shape=(block,...]
where the time goes in v4:
time: 76.5 us; the launch traced here: 76.3 us
  Pallas kernels  75.7 us (99%)
    pallas_call x1, Pallas kernels, local(): pl.pallas_call(functools.partial(gram_kernel, tokens), out_shape=(block,...  66.7 us
    pallas_call x1, Pallas kernels, local(): pl.pallas_call(solve_kernel, out_shape=(result, result), name='solve')  8.96 us

profile of v4, /device:TPU:17, one launch (start us, length us, event | category | flops | bytes accessed | tf_op | source)
XLA Modules:
  0.0 76.3 jit_solution(1073890459223385444)
XLA Ops:
  0.6 66.7 %grams.1 = (f32[128,128]{1,0:T(8,128)}, f32[128,128]{1,0:T(8,128)}, f32[128,128]{1,0:T(8,128)}, f32[2,8,128]{2,1,0:T(8,128)}) custom-call(bf16[192,2,4096]{2,1,0:T(2,128)(2,1)} %x_hbm.1, f32[2]{0:T(128)} %damping_ref.1), custom_call_target="tpu_custom_call" | custom-call | tf_op jit(solution)/shard_map/grams/pallas_call | solution.py:518
  67.3 9.0 %solve.1 = (f32[1,128,128]{2,1,0:T(8,128)}, f32[1,128,128]{2,1,0:T(8,128)}) custom-call(f32[128,128]{1,0:T(8,128)} %get-tuple-element.6.diagonal_ref, f32[128,128]{1,0:T(8,128)} %get-tuple-element.7.cross_ref, f32[128,128]{1,0:T(8,128)} %get-tuple-element.8.following_ref, f32[2,8,128]{2,1,0:T(8,128)} %get-tuple-element.9.level_ref), custom_call_target="tpu_custom_call" | custom-call | tf_op jit(solution)/shard_map/solve/pallas_call | solution.py:563
